TPU v7x, 32 devices: a whole 2x2x4 slice. The times are simulated.
32 devices in a mesh: row: 8 (over z, y), col: 4 (over x, core).
Axes of the slice: x: 2, y: 2, z: 4, core: 2. Of those that a mesh axis runs over, the one named last changes fastest.
Arguments:
- spectra: bfloat16 [1024, 16, 128], P(('row', 'col')), may hold values from -4 to 4
- window_flags: int32 [1024, 64], P(('row', 'col')), may hold values 0 or 1
- pair_mask: int32 [1024, 1024], P('row', 'col'), may hold values 0 or 1
- misfit_weight: bfloat16 [16, 1024, 1024], P(None, 'row', 'col'), may hold values from 0.0099487305 to 0.099609375
- observed: bfloat16 [2, 16, 1024, 1024], P(None, None, 'row', 'col'), may hold values from -6 to 6
Outputs:
- grad_first: bfloat16 [1024, 16, 128], P(('row', 'col'))
- grad_second: bfloat16 [4, 256, 16, 128], P('col', 'row')
All inputs are finite; a program needn't handle non-finite values. No bound on the sum of `window_flags` or of `pair_mask` on one device may be relied on, other than what follows from the above.
Results may differ from a plain program's by a relative error of at most 0.019.
Values may be sent and summed in bfloat16 or wider, within the bound.
No kernel may reach another device: no remote copies, remote signals or barrier semaphores. Data moves between devices by JAX's collectives and lax.ppermute only.
A program may use at most 64 MiB of HBM per device.

v0:
```python
import functools
import math

import jax
import jax.numpy as jnp
from jax import lax
from jax.experimental import pallas as pl
from jax.experimental.pallas import tpu as pltpu
from jax.sharding import PartitionSpec as P


AXES = ("row", "col")
F32 = jnp.float32
BF16 = jnp.bfloat16
SPARE = 2 << 20
WAIT_FLOPS = 5 * 10**9
UNROLL = 8
CUTS = (0, 8, 16)
PARTS = len(CUTS) - 1
GROUP = 2


def place(ratio):
    row = lax.axis_index("row")
    return row // ratio, row % ratio, lax.axis_index("col")


def spread(col, cols):
    return col // 2 + (col % 2) * (cols // 2)


def unspread(plane, cols):
    return (2 * plane) % cols + (2 * plane) // cols


def at(slot, n):
    return pl.ds(pl.multiple_of(slot * n, n), n)


def kernel_call(body, outs, scratch, flops, args):
    shapes = [jax.ShapeDtypeStruct(*o) for o in outs]
    moved = sum(a.size * a.dtype.itemsize for a in (*args, *shapes))
    held = sum(math.prod(m.shape) * jnp.dtype(m.dtype).itemsize for m in scratch)
    near = pl.BlockSpec(memory_space=pltpu.VMEM)
    return pl.pallas_call(
        body,
        out_shape=shapes,
        in_specs=[near] * len(args),
        out_specs=[near] * len(outs),
        scratch_shapes=scratch,
        compiler_params=pltpu.CompilerParams(vmem_limit_bytes=moved + held + SPARE),
        cost_estimate=pl.CostEstimate(
            flops=flops, bytes_accessed=moved, transcendentals=0
        ),
    )(*args)


def bits_body(flags, out):
    half, width = flags.shape[1], out.shape[1]
    copies = lax.broadcasted_iota(jnp.int32, (half, width), 1) % half
    copies = (copies == lax.broadcasted_iota(jnp.int32, (half, width), 0)).astype(BF16)
    out[...] = jnp.dot(flags[...].astype(F32).astype(BF16), copies, preferred_element_type=F32)


def flag_body(spectra, both, out, wide):
    n, freqs, width = spectra.shape
    wide[...] = spectra[...].astype(F32).reshape(n * freqs, width)
    for f in range(freqs):
        out[f] = (wide[pl.ds(f, n, stride=freqs), :] * both[...]).astype(BF16)


def join_body(ratio, bounds, own, mate, *outs):
    core = place(ratio)[2] % 2
    n = own.shape[1]
    whole = outs[0]
    whole[:, at(core, n), :] = own[...]
    whole[:, at(1 - core, n), :] = mate[...]
    for q, out in enumerate(outs[1:]):
        part = slice(bounds[q], bounds[q + 1])
        out[:, at(core, n), :] = own[part]
        out[:, at(1 - core, n), :] = mate[part]


def stack_body(*refs):
    pieces, out = refs[:-1], refs[-1]
    n = pieces[0].shape[1]
    for k, value in enumerate(pieces):
        out[:, k * n : (k + 1) * n, :] = value[...]


def unroll_of(steps):
    return max(u for u in range(1, UNROLL + 1) if steps % u == 0)


def turned(value, width):
    lane = lax.broadcasted_iota(jnp.int32, value.shape, 1)
    sign = jnp.where(lane < width // 2, 1.0, -1.0).astype(F32)
    return pltpu.roll(value.astype(F32), width // 2, 1) * sign


def side_stack(left, f):
    mine = left[f]
    return jnp.concatenate([mine, turned(mine, mine.shape[1]).astype(BF16)], axis=0)


def taken(pieces, k, n):
    return pieces[k][...] if len(pieces) > 1 else pieces[0][:, k * n : (k + 1) * n, :]


def pair_body(cols, ratio, d, start, *refs):
    half = cols // 2
    side, rest = refs[:half], refs[half:]
    pieces, rest = (rest[:1], rest[1:]) if d else (rest[:half], rest[half:])
    (mask, weight, observed), rest = rest[:3], rest[3:]
    earlier, rest = rest[:d], rest[d:]
    residuals, outs, (left, right, second) = rest[0], rest[1:-3], rest[-3:]
    plane, turn, col = place(ratio)
    freqs, rows, _ = left.shape
    n = rows // cols
    for k in range(half):
        left[:, at((col // 2) ^ k, 2 * n), :] = side[k][start : start + freqs]
        right[:, at(unspread(plane ^ k, cols) // 2, 2 * n), :] = taken(pieces, k, 2 * n)
    columns = at(turn ^ d, rows)
    last = d == ratio - 1

    def one(i, _):
        f = start + i
        stack = side_stack(left, i)
        cross = lax.dot_general(
            stack, right[i], (((1,), (1,)), ((), ())), preferred_element_type=F32
        )
        scale = mask[:, columns].astype(F32) * weight[f, :, columns].astype(F32)
        real = scale * (cross[:rows] - observed[0, f, :, columns].astype(F32))
        imag = scale * (cross[rows:] - observed[1, f, :, columns].astype(F32))
        residual = jnp.concatenate([real.astype(BF16), imag.astype(BF16)], axis=0)
        residuals[i] = residual
        sums = lax.dot_general(
            residual, stack, (((0,), (0,)), ((), ())), preferred_element_type=F32
        ).astype(BF16)
        if last:
            second[i, columns] = sums
        else:
            outs[0][i] = sums
        return 0

    lax.fori_loop(0, freqs, one, 0, unroll=unroll_of(freqs))
    if not last:
        return
    for e, block in enumerate(earlier):
        second[:, at(turn ^ e, rows), :] = block[...]
    kept, sent = outs[:cols], outs[cols:]
    for m in range(cols):
        slot = (plane ^ m) * ratio
        kept[m][...] = second[:, at(slot + turn, n), :]
        group, spot = divmod(m, GROUP)
        for e in range(1, ratio):
            there = second[:, at(slot + (turn ^ e), n), :]
            sent[group * (ratio - 1) + e - 1][:, spot * n : (spot + 1) * n, :] = there


def first_body(cols, ratio, parts, *refs):
    half = cols // 2
    per = half + 2 * ratio - 1
    groups, rest = [refs[q * per : (q + 1) * per] for q in range(parts)], refs[parts * per :]
    odd, evens, (right, first) = rest[0], rest[1:-2], rest[-2:]
    plane, _, col = place(ratio)
    _, rows, width = first.shape
    n = rows // cols
    start = 0
    for group in groups:
        pieces, residuals = group[: half + ratio - 1], group[half + ratio - 1 :]
        pieces = [pieces[:half], *([p] for p in pieces[half:])]
        size = residuals[0].shape[0]
        for d in range(ratio):
            for k in range(half):
                slot = d * half + unspread(plane ^ k, cols) // 2
                right[:size, at(slot, 2 * n), :] = taken(pieces[d], k, 2 * n)

        def one(i, _, residuals=residuals, start=start):
            both = 0.0
            for d in range(ratio):
                other = right[i, d * rows : (d + 1) * rows]
                both += jnp.dot(residuals[d][i], other, preferred_element_type=F32)
            first[start + i] = (both[:rows] - turned(both[rows:], width)).astype(BF16)
            return 0

        lax.fori_loop(0, size, one, 0, unroll=unroll_of(size))
        start += size
    for k in range(half):
        evens[k][...] = first[:, at(col ^ (2 * k), n), :]
        odd[:, k * n : (k + 1) * n, :] = first[:, at(col ^ (2 * k + 1), n), :]


def fold_body(spots, *refs):
    terms, out = refs[:-1], refs[-1]
    n = out.shape[1]
    total = 0.0
    for spot, term in zip(spots, terms):
        total += term[:, spot * n : (spot + 1) * n, :].astype(F32)
    out[...] = total.astype(BF16)


def finish_body(count, parts, *refs):
    outs, wide = refs[-3:-1], refs[-1]
    n, freqs, width = outs[0].shape
    groups = [refs[:count]] + [refs[count + q : -3 : parts] for q in range(parts)]
    for out, sets in ((outs[0], groups[:1]), (outs[1], groups[1:])):
        f = 0
        for terms in sets:
            for i in range(terms[0].shape[0]):
                total = 0.0
                for term in terms:
                    total += term[i, :n].astype(F32)
                wide[pl.ds(f, n, stride=freqs), :] = total
                f += 1
        out[...] = wide[...].reshape(n, freqs, width).astype(BF16)


def per_device(row_count, cols, spectra, window_flags, pair_mask, misfit_weight, observed):
    ratio = row_count // cols
    half = cols // 2
    n, freqs, width = spectra.shape
    rows = cols * n
    bounds = [freqs * cut // CUTS[-1] for cut in CUTS]
    sizes = [b - a for a, b in zip(bounds, bounds[1:])]

    def send(value, where):
        pairs = []
        for row in range(row_count):
            for col in range(cols):
                plane, turn, to = where(row // ratio, row % ratio, col)
                pairs.append((row * cols + col, (plane * ratio + turn) * cols + to))
        return lax.ppermute(value, AXES, pairs)

    def piece(size, count=1):
        return ((size, count * n, width), BF16)

    (both,) = kernel_call(
        bits_body, [((n, width), F32)], [], WAIT_FLOPS, (window_flags,)
    )
    (own,) = kernel_call(
        flag_body,
        [piece(freqs)],
        [pltpu.VMEM((n * freqs, width), F32)],
        WAIT_FLOPS,
        (spectra, both),
    )
    mate = send(own, lambda z, t, c: (z, t, c ^ 1))
    chip, *chips = kernel_call(
        functools.partial(join_body, ratio, bounds),
        [piece(freqs, 2)] + [piece(size, 2) for size in sizes],
        [],
        own.size,
        (own, mate),
    )
    side = [chip] + [
        send(chip, lambda z, t, c: (z, t, c ^ (2 * k))) for k in range(1, half)
    ]
    first_args, second_args = [], []
    for q, size in enumerate(sizes):
        pieces = [
            send(chips[q], lambda z, t, c: (spread(c, cols) ^ k, t, z))
            for k in range(half)
        ]
        (stack,) = kernel_call(stack_body, [piece(size, cols)], [], own.size, pieces)
        for d in range(1, ratio):
            pieces.append(send(stack, lambda z, t, c: (z, t ^ d, c)))
        blocks, residuals = [], []
        groups = cols // GROUP
        for d in range(ratio):
            last = d == ratio - 1
            results = [piece(size)] * cols + [piece(size, GROUP)] * (groups * (ratio - 1))
            near = pieces[half + d - 1 : half + d] if d else pieces[:half]
            found, *outs = kernel_call(
                functools.partial(pair_body, cols, ratio, d, bounds[q]),
                [((size, 2 * rows, rows), BF16)] + (results if last else [piece(size, cols)]),
                [
                    pltpu.VMEM((size, rows, width), BF16),
                    pltpu.VMEM((size, rows, width), BF16),
                    pltpu.VMEM((size, rows * ratio, width), BF16),
                ],
                8 * size * rows * rows * width,
                (*side, *near, pair_mask, misfit_weight, observed, *blocks),
            )
            residuals.append(found)
            blocks += outs
        first_args += [*pieces, *residuals]
        kept, sent = blocks[ratio - 1 :][:cols], blocks[ratio - 1 :][cols:]
        back = [[] for _ in range(groups)]
        for g in range(groups):
            for d in range(1, ratio):
                value = sent[g * (ratio - 1) + d - 1]
                there = send(value, lambda z, t, c: (z, t ^ d, c))
                back[g].append(there)
        second_args.append([kept[0], *back[0]])
        for m in range(1, cols):
            spots = (0,) + (m % GROUP,) * (ratio - 1)
            (folded,) = kernel_call(
                functools.partial(fold_body, spots),
                [piece(size)],
                [],
                size * n,
                (kept[m], *back[m // GROUP]),
            )
            there = send(folded, lambda z, t, c: (z ^ m, t, c))
            second_args[q].append(there)

    odd, *evens = kernel_call(
        functools.partial(first_body, cols, ratio, PARTS),
        [piece(freqs, half)] + [piece(freqs)] * half,
        [
            pltpu.VMEM((max(sizes), rows * ratio, width), BF16),
            pltpu.VMEM((freqs, rows, width), BF16),
        ],
        4 * freqs * rows * rows * ratio * width,
        first_args,
    )
    odd = send(odd, lambda z, t, c: (z, t, c ^ 1))
    first_terms = [evens[0], odd]
    for k in range(1, half):
        (folded,) = kernel_call(
            functools.partial(fold_body, (0, k)), [piece(freqs)], [], n, (evens[k], odd)
        )
        there = send(folded, lambda z, t, c: (z, t, c ^ (2 * k)))
        first_terms.append(there)

    grad_first, grad_second = kernel_call(
        functools.partial(finish_body, len(first_terms), PARTS),
        [((n, freqs, width), BF16)] * 2,
        [pltpu.VMEM((n * freqs, width), F32)],
        cols * spectra.size,
        first_terms + [term for terms in zip(*second_args) for term in terms],
    )
    return grad_first, grad_second[None]


def solution(mesh):
    placed = (
        P(AXES, None, None),
        P(AXES, None),
        P("row", "col"),
        P(None, "row", "col"),
        P(None, None, "row", "col"),
    )
    row_count, cols = mesh.shape["row"], mesh.shape["col"]
    ratio = row_count // cols
    for count in (cols, ratio):
        assert count & (count - 1) == 0 and cols % GROUP == 0 and cols > 1, "mesh sizes"

    def body(*args):
        return per_device(row_count, cols, *args)

    return jax.shard_map(
        body,
        mesh=mesh,
        in_specs=placed,
        out_specs=(P(AXES, None, None), P("col", "row", None, None)),
        check_vma=False,
    )
```

profile of v0, /device:TPU:0, one launch (start us, length us, event | category | flops | bytes accessed | tf_op | source)
XLA Modules:
  0.0 57.2 jit_solution(16254753436899426710)
XLA Ops:
  0.6 0.7 %copy-done.4 = s32[32,64]{1,0:T(8,128)S(1)} copy-done((s32[32,64]{1,0:T(8,128)S(1)}, s32[32,64]{1,0:T(8,128)}, u32[]{:S(2)}) %copy-start.4) | copy-done | bytes 8216
  1.7 0.6 collective-permute-start
  2.2 1.0 %collective-permute-done.mate = bf16[16,32,128]{2,1,0:T(8,128)(2,1)S(1)} collective-permute-done((bf16[16,32,128]{2,1,0:T(8,128)(2,1)S(1)}, bf16[16,32,128]{2,1,0:T(8,128)(2,1)S(1)}, u32[]{:S(2)}, u32[]{:S(2)}) %collective-permute-start) | collective-permute-done | bytes 131104 | tf_op jit(solution)/shard_map/ppermute | solution.py:233
  3.3 3.0 %collective-permute-start.6 = (bf16[8,64,128]{2,1,0:T(8,128)(2,1)S(1)}, bf16[8,64,128]{2,1,0:T(8,128)(2,1)S(1)}, u32[]{:S(2)}, u32[]{:S(2)}) collective-permute-start(bf16[8,64,128]{2,1,0:T(8,128)(2,1)S(1)} %get-tuple-element.33), channel_id=1, source_target_pairs={{0,8},{1,24},{2,0},{3,16},{4,12},{5,28},{6,4},{7,20},{8,9},{9,25},... | collective-permute-start | bytes 393224 | tf_op jit(solution)/shard_map/ppermute | solution.py:233
  6.3 0.7 %collective-permute-start.5 = (bf16[8,64,128]{2,1,0:T(8,128)(2,1)S(1)}, bf16[8,64,128]{2,1,0:T(8,128)(2,1)S(1)}, u32[]{:S(2)}, u32[]{:S(2)}) collective-permute-start(bf16[8,64,128]{2,1,0:T(8,128)(2,1)S(1)} %get-tuple-element.33), channel_id=1, source_target_pairs={{0,0},{1,16},{2,8},{3,24},{4,4},{5,20},{6,12},{7,28},{8,1},{9,17},... | collective-permute-start | bytes 393224 | tf_op jit(solution)/shard_map/ppermute | solution.py:233
  6.9 5.1 %collective-permute-start.2 = (bf16[8,64,128]{2,1,0:T(8,128)(2,1)S(1)}, bf16[8,64,128]{2,1,0:T(8,128)(2,1)S(1)}, u32[]{:S(2)}, u32[]{:S(2)}) collective-permute-start(bf16[8,64,128]{2,1,0:T(8,128)(2,1)S(1)} %get-tuple-element.28), channel_id=1, source_target_pairs={{0,8},{1,24},{2,0},{3,16},{4,12},{5,28},{6,4},{7,20},{8,9},{9,25},... | collective-permute-start | bytes 393224 | tf_op jit(solution)/shard_map/ppermute | solution.py:233
  12.0 0.7 %collective-permute-start.1 = (bf16[8,64,128]{2,1,0:T(8,128)(2,1)S(1)}, bf16[8,64,128]{2,1,0:T(8,128)(2,1)S(1)}, u32[]{:S(2)}, u32[]{:S(2)}) collective-permute-start(bf16[8,64,128]{2,1,0:T(8,128)(2,1)S(1)} %get-tuple-element.28), channel_id=1, source_target_pairs={{0,0},{1,16},{2,8},{3,24},{4,4},{5,20},{6,12},{7,28},{8,1},{9,17},... | collective-permute-start | bytes 393224 | tf_op jit(solution)/shard_map/ppermute | solution.py:233
  12.7 2.9 %collective-permute-start.4 = (bf16[16,64,128]{2,1,0:T(8,128)(2,1)S(1)}, bf16[16,64,128]{2,1,0:T(8,128)(2,1)S(1)}, u32[]{:S(2)}, u32[]{:S(2)}) collective-permute-start(bf16[16,64,128]{2,1,0:T(8,128)(2,1)S(1)} %get-tuple-element.29.refs_0_), channel_id=1, source_target_pairs={{0,2},{1,3},{2,0},{3,1},{4,6},{5,7},{6,4},{7,5},{8,10},{9,11},{10,... | collective-permute-start | bytes 786440 | tf_op jit(solution)/shard_map/ppermute | solution.py:233
  15.6 1.6 %collective-permute-start.7 = (bf16[8,128,128]{2,1,0:T(8,128)(2,1)S(1)}, bf16[8,128,128]{2,1,0:T(8,128)(2,1)S(1)}, u32[]{:S(2)}, u32[]{:S(2)}) collective-permute-start(bf16[8,128,128]{2,1,0:T(8,128)(2,1)S(1)} %shard_map.74), channel_id=1, source_target_pairs={{0,4},{1,5},{2,6},{3,7},{4,0},{5,1},{6,2},{7,3},{8,12},{9,13},{10,... | collective-permute-start | bytes 786440 | tf_op jit(solution)/shard_map/ppermute | solution.py:233
  17.2 0.6 collective-permute-start.3
  17.8 5.9 %collective-permute-done.4.refs_1_ = bf16[16,64,128]{2,1,0:T(8,128)(2,1)S(1)} collective-permute-done((bf16[16,64,128]{2,1,0:T(8,128)(2,1)S(1)}, bf16[16,64,128]{2,1,0:T(8,128)(2,1)S(1)}, u32[]{:S(2)}, u32[]{:S(2)}) %collective-permute-start.4) | collective-permute-done | bytes 262176 | tf_op jit(solution)/shard_map/ppermute | solution.py:233
  23.7 0.9 %shard_map.75 = (bf16[8,256,128]{2,1,0:T(8,128)(2,1)S(1)}, bf16[8,128,128]{2,1,0:T(8,128)(2,1)S(1)}) custom-call(bf16[16,64,128]{2,1,0:T(8,128)(2,1)S(1)} %get-tuple-element.29.refs_0_, bf16[16,64,128]{2,1,0:T(8,128)(2,1)S(1)} %collective-permute-done.4.refs_1_, bf16[8,64,128]{2,1,0:T(8,128)(2,1)S(1)} %collective-permute-done.5.refs_0_.refs_2_.refs_5_, ...), custom_call_target="tpu_custom_call" | custom-call | flops 134217728 | bytes 4849664 | tf_op jit(solution)/shard_map/pallas_call | solution.py:45
  24.6 0.9 %shard_map.72 = (bf16[8,256,128]{2,1,0:T(8,128)(2,1)S(1)}, bf16[8,128,128]{2,1,0:T(8,128)(2,1)S(1)}) custom-call(bf16[16,64,128]{2,1,0:T(8,128)(2,1)S(1)} %get-tuple-element.29.refs_0_, bf16[16,64,128]{2,1,0:T(8,128)(2,1)S(1)} %collective-permute-done.4.refs_1_, bf16[8,64,128]{2,1,0:T(8,128)(2,1)S(1)} %collective-permute-done.1.refs_0_.refs_2_, ...), custom_call_target="tpu_custom_call" | custom-call | flops 134217728 | bytes 4849664 | tf_op jit(solution)/shard_map/pallas_call | solution.py:45
  25.5 1.0 %shard_map.76 = (bf16[8,256,128]{2,1,0:T(8,128)(2,1)S(1)}, bf16[8,32,128]{2,1,0:T(8,128)(2,1)S(1)}, bf16[8,32,128]{2,1,0:T(8,128)(2,1)S(1)}, bf16[8,32,128]{2,1,...) custom-call(bf16[16,64,128]{2,1,0:T(8,128)(2,1)S(1)} %get-tuple-elem, ...), custom_call_target="tpu_custom_call" | custom-call | flops 134217728 | bytes 5373952 | tf_op jit(solution)/shard_map/pallas_call | solution.py:45
  26.5 2.5 %collective-permute-done.3.refs_2_ = bf16[8,128,128]{2,1,0:T(8,128)(2,1)S(1)} collective-permute-done((bf16[8,128,128]{2,1,0:T(8,128)(2,1)S(1)}, bf16[8,128,128]{2,1,0:T(8,128)(2,1)S(1)}, u32[]{:S(2)}, u32[]{:S(2)}) %collective-permute-start.3) | collective-permute-done | bytes 262176 | tf_op jit(solution)/shard_map/ppermute | solution.py:233
  29.0 1.0 %shard_map.73 = (bf16[8,256,128]{2,1,0:T(8,128)(2,1)S(1)}, bf16[8,32,128]{2,1,0:T(8,128)(2,1)S(1)}, bf16[8,32,128]{2,1,0:T(8,128)(2,1)S(1)}, bf16[8,32,128]{2,1,...) custom-call(bf16[16,64,128]{2,1,0:T(8,128)(2,1)S(1)} %get-tuple-elem, ...), custom_call_target="tpu_custom_call" | custom-call | flops 134217728 | bytes 5373952 | tf_op jit(solution)/shard_map/pallas_call | solution.py:45
  30.0 0.9 %shard_map.77 = (bf16[16,64,128]{2,1,0:T(8,128)(2,1)S(1)}, bf16[16,32,128]{2,1,0:T(8,128)(2,1)S(1)}, bf16[16,32,128]{2,1,0:T(8,128)(2,1)S(1)}) custom-call(bf16[8,64,128]{2,1,0:T(8,128)(2,1)S(1)} %collective-permute-done.1.refs_0_.refs_2_, bf16[8,64,128]{2,1,0:T(8,128)(2,1)S(1)} %collective-permute-done.2.refs_1_.refs_3_, ...), custom_call_target="tpu_custom_call" | custom-call | flops 268435456 | bytes 3670016 | tf_op jit(solution)/shard_map/pallas_call | solution.py:45
  30.9 1.4 %collective-permute-start.8 = (bf16[16,64,128]{2,1,0:T(8,128)(2,1)S(1)}, bf16[16,64,128]{2,1,0:T(8,128)(2,1)S(1)}, u32[]{:S(2)}, u32[]{:S(2)}) collective-permute-start(bf16[16,64,128]{2,1,0:T(8,128)(2,1)S(1)} %get-tuple-element.38), channel_id=1, source_target_pairs={{0,1},{1,0},{2,3},{3,2},{4,5},{5,4},{6,7},{7,6},{8,9},{9,8},{10,11... | collective-permute-start | bytes 786440 | tf_op jit(solution)/shard_map/ppermute | solution.py:233
  32.2 1.5 %collective-permute-start.11 = (bf16[8,64,128]{2,1,0:T(8,128)(2,1)S(1)}, bf16[8,64,128]{2,1,0:T(8,128)(2,1)S(1)}, u32[]{:S(2)}, u32[]{:S(2)}) collective-permute-start(bf16[8,64,128]{2,1,0:T(8,128)(2,1)S(1)} %get-tuple-element.43), channel_id=1, source_target_pairs={{0,4},{1,5},{2,6},{3,7},{4,0},{5,1},{6,2},{7,3},{8,12},{9,13},{10,... | collective-permute-start | bytes 393224 | tf_op jit(solution)/shard_map/ppermute | solution.py:233
  33.8 0.5 collective-permute-start.16
  34.3 1.5 %collective-permute-start.10 = (bf16[8,64,128]{2,1,0:T(8,128)(2,1)S(1)}, bf16[8,64,128]{2,1,0:T(8,128)(2,1)S(1)}, u32[]{:S(2)}, u32[]{:S(2)}) collective-permute-start(bf16[8,64,128]{2,1,0:T(8,128)(2,1)S(1)} %get-tuple-element.42), channel_id=1, source_target_pairs={{0,4},{1,5},{2,6},{3,7},{4,0},{5,1},{6,2},{7,3},{8,12},{9,13},{10,... | collective-permute-start | bytes 393224 | tf_op jit(solution)/shard_map/ppermute | solution.py:233
  35.8 0.5 collective-permute-start.14
  36.3 2.3 %collective-permute-done.11.refs_1_.refs_6_ = bf16[8,64,128]{2,1,0:T(8,128)(2,1)S(1)} collective-permute-done((bf16[8,64,128]{2,1,0:T(8,128)(2,1)S(1)}, bf16[8,64,128]{2,1,0:T(8,128)(2,1)S(1)}, u32[]{:S(2)}, u32[]{:S(2)}) %collective-permute-start.11) | collective-permute-done | bytes 131104 | tf_op jit(solution)/shard_map/ppermute | solution.py:233
  38.7 2.7 %collective-permute-done.16.refs_1_ = bf16[8,64,128]{2,1,0:T(8,128)(2,1)S(1)} collective-permute-done((bf16[8,64,128]{2,1,0:T(8,128)(2,1)S(1)}, bf16[8,64,128]{2,1,0:T(8,128)(2,1)S(1)}, u32[]{:S(2)}, u32[]{:S(2)}) %collective-permute-start.16) | collective-permute-done | bytes 131104 | tf_op jit(solution)/shard_map/ppermute | solution.py:233
  41.4 1.7 %collective-permute-start.17 = (bf16[8,32,128]{2,1,0:T(8,128)(2,1)S(1)}, bf16[8,32,128]{2,1,0:T(8,128)(2,1)S(1)}, u32[]{:S(2)}, u32[]{:S(2)}) collective-permute-start(bf16[8,32,128]{2,1,0:T(8,128)(2,1)S(1)} %shard_map.82), channel_id=1, source_target_pairs={{0,16},{1,17},{2,18},{3,19},{4,20},{5,21},{6,22},{7,23},{8,24},{9,... | collective-permute-start | bytes 196616 | tf_op jit(solution)/shard_map/ppermute | solution.py:233
  43.5 0.7 %collective-permute-done.10.refs_1_.refs_5_ = bf16[8,64,128]{2,1,0:T(8,128)(2,1)S(1)} collective-permute-done((bf16[8,64,128]{2,1,0:T(8,128)(2,1)S(1)}, bf16[8,64,128]{2,1,0:T(8,128)(2,1)S(1)}, u32[]{:S(2)}, u32[]{:S(2)}) %collective-permute-start.10) | collective-permute-done | bytes 131104 | tf_op jit(solution)/shard_map/ppermute | solution.py:233
  44.2 3.0 %collective-permute-start.19 = (bf16[8,32,128]{2,1,0:T(8,128)(2,1)S(1)}, bf16[8,32,128]{2,1,0:T(8,128)(2,1)S(1)}, u32[]{:S(2)}, u32[]{:S(2)}) collective-permute-start(bf16[8,32,128]{2,1,0:T(8,128)(2,1)S(1)} %shard_map.84), channel_id=1, source_target_pairs={{0,24},{1,25},{2,26},{3,27},{4,28},{5,29},{6,30},{7,31},{8,16},{9,... | collective-permute-start | bytes 196616 | tf_op jit(solution)/shard_map/ppermute | solution.py:233
  47.4 2.8 %collective-permute-start.15 = (bf16[8,32,128]{2,1,0:T(8,128)(2,1)S(1)}, bf16[8,32,128]{2,1,0:T(8,128)(2,1)S(1)}, u32[]{:S(2)}, u32[]{:S(2)}) collective-permute-start(bf16[8,32,128]{2,1,0:T(8,128)(2,1)S(1)} %shard_map.81), channel_id=1, source_target_pairs={{0,16},{1,17},{2,18},{3,19},{4,20},{5,21},{6,22},{7,23},{8,24},{9,... | collective-permute-start | bytes 196616 | tf_op jit(solution)/shard_map/ppermute | solution.py:233
  50.2 1.7 %collective-permute-start.18 = (bf16[8,32,128]{2,1,0:T(8,128)(2,1)S(1)}, bf16[8,32,128]{2,1,0:T(8,128)(2,1)S(1)}, u32[]{:S(2)}, u32[]{:S(2)}) collective-permute-start(bf16[8,32,128]{2,1,0:T(8,128)(2,1)S(1)} %shard_map.83), channel_id=1, source_target_pairs={{0,24},{1,25},{2,26},{3,27},{4,28},{5,29},{6,30},{7,31},{8,16},{9,... | collective-permute-start | bytes 196616 | tf_op jit(solution)/shard_map/ppermute | solution.py:233
  51.9 1.4 %collective-permute-done.15.refs_9_ = bf16[8,32,128]{2,1,0:T(8,128)(2,1)S(1)} collective-permute-done((bf16[8,32,128]{2,1,0:T(8,128)(2,1)S(1)}, bf16[8,32,128]{2,1,0:T(8,128)(2,1)S(1)}, u32[]{:S(2)}, u32[]{:S(2)}) %collective-permute-start.15) | collective-permute-done | bytes 65568 | tf_op jit(solution)/shard_map/ppermute | solution.py:233
  53.3 2.9 %collective-permute-done.18.refs_11_ = bf16[8,32,128]{2,1,0:T(8,128)(2,1)S(1)} collective-permute-done((bf16[8,32,128]{2,1,0:T(8,128)(2,1)S(1)}, bf16[8,32,128]{2,1,0:T(8,128)(2,1)S(1)}, u32[]{:S(2)}, u32[]{:S(2)}) %collective-permute-start.18) | collective-permute-done | bytes 65568 | tf_op jit(solution)/shard_map/ppermute | solution.py:233
  56.2 0.9 %shard_map.85 = (bf16[32,16,128]{2,1,0:T(8,128)(2,1)}, bf16[32,16,128]{2,1,0:T(8,128)(2,1)}) custom-call(bf16[16,32,128]{2,1,0:T(8,128)(2,1)S(1)} %get-tuple-element.37.refs_0_, bf16[16,64,128]{2,1,0:T(8,128)(2,1)S(1)} %collective-permute-done.8.refs_1_, bf16[16,32,128]{2,1,0:T(8,128)(2,1)S(1)} %collective-permute-done.9.refs_2_, ...), custom_call_target="tpu_custom_call" | custom-call | flops 262144 | bytes 1572864 | tf_op jit(solution)/shard_map/pallas_call | solution.py:45
  (36 shorter events, 1.0 us)
Async XLA Ops:
  0.6 0.9 %copy-start.3 = (bf16[32,16,128]{2,1,0:T(8,128)(2,1)S(1)}, bf16[32,16,128]{2,1,0:T(8,128)(2,1)}, u32[]{:S(2)}) copy-start(bf16[32,16,128]{2,1,0:T(8,128)(2,1)} %spectra.1) | copy-start | bytes 393220
  0.6 0.8 %copy-start.4 = (s32[32,64]{1,0:T(8,128)S(1)}, s32[32,64]{1,0:T(8,128)}, u32[]{:S(2)}) copy-start(s32[32,64]{1,0:T(8,128)} %flags.1) | copy-start | bytes 24580
  1.6 22.2 %copy-start = (bf16[2,16,128,256]{3,2,1,0:T(8,128)(2,1)S(1)}, bf16[2,16,128,256]{3,2,1,0:T(8,128)(2,1)}, u32[]{:S(2)}) copy-start(bf16[2,16,128,256]{3,2,1,0:T(8,128)(2,1)} %refs_5_.7) | copy-start | bytes 6291460
  1.6 22.2 %copy-start.1 = (bf16[16,128,256]{2,1,0:T(8,128)(2,1)S(1)}, bf16[16,128,256]{2,1,0:T(8,128)(2,1)}, u32[]{:S(2)}) copy-start(bf16[16,128,256]{2,1,0:T(8,128)(2,1)} %refs_4_.7) | copy-start | bytes 3145732
  1.6 22.2 %copy-start.2 = (s32[128,256]{1,0:T(8,128)S(1)}, s32[128,256]{1,0:T(8,128)}, u32[]{:S(2)}) copy-start(s32[128,256]{1,0:T(8,128)} %refs_3_.3) | copy-start | bytes 393220
  1.7 1.5 %collective-permute-start = (bf16[16,32,128]{2,1,0:T(8,128)(2,1)S(1)}, bf16[16,32,128]{2,1,0:T(8,128)(2,1)S(1)}, u32[]{:S(2)}, u32[]{:S(2)}) collective-permute-start(bf16[16,32,128]{2,1,0:T(8,128)(2,1)S(1)} %shard_map.69.own), channel_id=1, source_target_pairs={{0,1},{1,0},{2,3},{3,2},{4,5},{5,4},{6,7},{7,6},{8,9},{9,8},{10,11... | collective-permute-start | bytes 393224 | tf_op jit(solution)/shard_map/ppermute | solution.py:233
  3.3 12.3 %collective-permute-start.6 = (bf16[8,64,128]{2,1,0:T(8,128)(2,1)S(1)}, bf16[8,64,128]{2,1,0:T(8,128)(2,1)S(1)}, u32[]{:S(2)}, u32[]{:S(2)}) collective-permute-start(bf16[8,64,128]{2,1,0:T(8,128)(2,1)S(1)} %get-tuple-element.33), channel_id=1, source_target_pairs={{0,8},{1,24},{2,0},{3,16},{4,12},{5,28},{6,4},{7,20},{8,9},{9,25},... | collective-permute-start | bytes 393224 | tf_op jit(solution)/shard_map/ppermute | solution.py:233
  6.3 9.3 %collective-permute-start.5 = (bf16[8,64,128]{2,1,0:T(8,128)(2,1)S(1)}, bf16[8,64,128]{2,1,0:T(8,128)(2,1)S(1)}, u32[]{:S(2)}, u32[]{:S(2)}) collective-permute-start(bf16[8,64,128]{2,1,0:T(8,128)(2,1)S(1)} %get-tuple-element.33), channel_id=1, source_target_pairs={{0,0},{1,16},{2,8},{3,24},{4,4},{5,20},{6,12},{7,28},{8,1},{9,17},... | collective-permute-start | bytes 393224 | tf_op jit(solution)/shard_map/ppermute | solution.py:233
  6.9 10.3 %collective-permute-start.2 = (bf16[8,64,128]{2,1,0:T(8,128)(2,1)S(1)}, bf16[8,64,128]{2,1,0:T(8,128)(2,1)S(1)}, u32[]{:S(2)}, u32[]{:S(2)}) collective-permute-start(bf16[8,64,128]{2,1,0:T(8,128)(2,1)S(1)} %get-tuple-element.28), channel_id=1, source_target_pairs={{0,8},{1,24},{2,0},{3,16},{4,12},{5,28},{6,4},{7,20},{8,9},{9,25},... | collective-permute-start | bytes 393224 | tf_op jit(solution)/shard_map/ppermute | solution.py:233
  12.0 5.2 %collective-permute-start.1 = (bf16[8,64,128]{2,1,0:T(8,128)(2,1)S(1)}, bf16[8,64,128]{2,1,0:T(8,128)(2,1)S(1)}, u32[]{:S(2)}, u32[]{:S(2)}) collective-permute-start(bf16[8,64,128]{2,1,0:T(8,128)(2,1)S(1)} %get-tuple-element.28), channel_id=1, source_target_pairs={{0,0},{1,16},{2,8},{3,24},{4,4},{5,20},{6,12},{7,28},{8,1},{9,17},... | collective-permute-start | bytes 393224 | tf_op jit(solution)/shard_map/ppermute | solution.py:233
  12.7 11.1 %collective-permute-start.4 = (bf16[16,64,128]{2,1,0:T(8,128)(2,1)S(1)}, bf16[16,64,128]{2,1,0:T(8,128)(2,1)S(1)}, u32[]{:S(2)}, u32[]{:S(2)}) collective-permute-start(bf16[16,64,128]{2,1,0:T(8,128)(2,1)S(1)} %get-tuple-element.29.refs_0_), channel_id=1, source_target_pairs={{0,2},{1,3},{2,0},{3,1},{4,6},{5,7},{6,4},{7,5},{8,10},{9,11},{10,... | collective-permute-start | bytes 786440 | tf_op jit(solution)/shard_map/ppermute | solution.py:233
  15.6 9.9 %collective-permute-start.7 = (bf16[8,128,128]{2,1,0:T(8,128)(2,1)S(1)}, bf16[8,128,128]{2,1,0:T(8,128)(2,1)S(1)}, u32[]{:S(2)}, u32[]{:S(2)}) collective-permute-start(bf16[8,128,128]{2,1,0:T(8,128)(2,1)S(1)} %shard_map.74), channel_id=1, source_target_pairs={{0,4},{1,5},{2,6},{3,7},{4,0},{5,1},{6,2},{7,3},{8,12},{9,13},{10,... | collective-permute-start | bytes 786440 | tf_op jit(solution)/shard_map/ppermute | solution.py:233
  17.2 11.8 %collective-permute-start.3 = (bf16[8,128,128]{2,1,0:T(8,128)(2,1)S(1)}, bf16[8,128,128]{2,1,0:T(8,128)(2,1)S(1)}, u32[]{:S(2)}, u32[]{:S(2)}) collective-permute-start(bf16[8,128,128]{2,1,0:T(8,128)(2,1)S(1)} %shard_map.71), channel_id=1, source_target_pairs={{0,4},{1,5},{2,6},{3,7},{4,0},{5,1},{6,2},{7,3},{8,12},{9,13},{10,... | collective-permute-start | bytes 786440 | tf_op jit(solution)/shard_map/ppermute | solution.py:233
  30.9 12.3 %collective-permute-start.8 = (bf16[16,64,128]{2,1,0:T(8,128)(2,1)S(1)}, bf16[16,64,128]{2,1,0:T(8,128)(2,1)S(1)}, u32[]{:S(2)}, u32[]{:S(2)}) collective-permute-start(bf16[16,64,128]{2,1,0:T(8,128)(2,1)S(1)} %get-tuple-element.38), channel_id=1, source_target_pairs={{0,1},{1,0},{2,3},{3,2},{4,5},{5,4},{6,7},{7,6},{8,9},{9,8},{10,11... | collective-permute-start | bytes 786440 | tf_op jit(solution)/shard_map/ppermute | solution.py:233
  32.2 6.4 %collective-permute-start.11 = (bf16[8,64,128]{2,1,0:T(8,128)(2,1)S(1)}, bf16[8,64,128]{2,1,0:T(8,128)(2,1)S(1)}, u32[]{:S(2)}, u32[]{:S(2)}) collective-permute-start(bf16[8,64,128]{2,1,0:T(8,128)(2,1)S(1)} %get-tuple-element.43), channel_id=1, source_target_pairs={{0,4},{1,5},{2,6},{3,7},{4,0},{5,1},{6,2},{7,3},{8,12},{9,13},{10,... | collective-permute-start | bytes 393224 | tf_op jit(solution)/shard_map/ppermute | solution.py:233
  33.8 7.7 %collective-permute-start.16 = (bf16[8,64,128]{2,1,0:T(8,128)(2,1)S(1)}, bf16[8,64,128]{2,1,0:T(8,128)(2,1)S(1)}, u32[]{:S(2)}, u32[]{:S(2)}) collective-permute-start(bf16[8,64,128]{2,1,0:T(8,128)(2,1)S(1)} %get-tuple-element.49), channel_id=1, source_target_pairs={{0,4},{1,5},{2,6},{3,7},{4,0},{5,1},{6,2},{7,3},{8,12},{9,13},{10,... | collective-permute-start | bytes 393224 | tf_op jit(solution)/shard_map/ppermute | solution.py:233
  34.3 10.0 %collective-permute-start.10 = (bf16[8,64,128]{2,1,0:T(8,128)(2,1)S(1)}, bf16[8,64,128]{2,1,0:T(8,128)(2,1)S(1)}, u32[]{:S(2)}, u32[]{:S(2)}) collective-permute-start(bf16[8,64,128]{2,1,0:T(8,128)(2,1)S(1)} %get-tuple-element.42), channel_id=1, source_target_pairs={{0,4},{1,5},{2,6},{3,7},{4,0},{5,1},{6,2},{7,3},{8,12},{9,13},{10,... | collective-permute-start | bytes 393224 | tf_op jit(solution)/shard_map/ppermute | solution.py:233
  35.8 11.5 %collective-permute-start.14 = (bf16[8,64,128]{2,1,0:T(8,128)(2,1)S(1)}, bf16[8,64,128]{2,1,0:T(8,128)(2,1)S(1)}, u32[]{:S(2)}, u32[]{:S(2)}) collective-permute-start(bf16[8,64,128]{2,1,0:T(8,128)(2,1)S(1)} %get-tuple-element.47), channel_id=1, source_target_pairs={{0,4},{1,5},{2,6},{3,7},{4,0},{5,1},{6,2},{7,3},{8,12},{9,13},{10,... | collective-permute-start | bytes 393224 | tf_op jit(solution)/shard_map/ppermute | solution.py:233
  38.6 8.8 %collective-permute-start.13 = (bf16[8,32,128]{2,1,0:T(8,128)(2,1)S(1)}, bf16[8,32,128]{2,1,0:T(8,128)(2,1)S(1)}, u32[]{:S(2)}, u32[]{:S(2)}) collective-permute-start(bf16[8,32,128]{2,1,0:T(8,128)(2,1)S(1)} %shard_map.80), channel_id=1, source_target_pairs={{0,8},{1,9},{2,10},{3,11},{4,12},{5,13},{6,14},{7,15},{8,0},{9,1},... | collective-permute-start | bytes 196616 | tf_op jit(solution)/shard_map/ppermute | solution.py:233
  41.4 8.7 %collective-permute-start.17 = (bf16[8,32,128]{2,1,0:T(8,128)(2,1)S(1)}, bf16[8,32,128]{2,1,0:T(8,128)(2,1)S(1)}, u32[]{:S(2)}, u32[]{:S(2)}) collective-permute-start(bf16[8,32,128]{2,1,0:T(8,128)(2,1)S(1)} %shard_map.82), channel_id=1, source_target_pairs={{0,16},{1,17},{2,18},{3,19},{4,20},{5,21},{6,22},{7,23},{8,24},{9,... | collective-permute-start | bytes 196616 | tf_op jit(solution)/shard_map/ppermute | solution.py:233
  43.2 13.0 %collective-permute-start.9 = (bf16[16,32,128]{2,1,0:T(8,128)(2,1)S(1)}, bf16[16,32,128]{2,1,0:T(8,128)(2,1)S(1)}, u32[]{:S(2)}, u32[]{:S(2)}) collective-permute-start(bf16[16,32,128]{2,1,0:T(8,128)(2,1)S(1)} %shard_map.78), channel_id=1, source_target_pairs={{0,2},{1,3},{2,0},{3,1},{4,6},{5,7},{6,4},{7,5},{8,10},{9,11},{10,... | collective-permute-start | bytes 393224 | tf_op jit(solution)/shard_map/ppermute | solution.py:233
  44.2 7.6 %collective-permute-start.19 = (bf16[8,32,128]{2,1,0:T(8,128)(2,1)S(1)}, bf16[8,32,128]{2,1,0:T(8,128)(2,1)S(1)}, u32[]{:S(2)}, u32[]{:S(2)}) collective-permute-start(bf16[8,32,128]{2,1,0:T(8,128)(2,1)S(1)} %shard_map.84), channel_id=1, source_target_pairs={{0,24},{1,25},{2,26},{3,27},{4,28},{5,29},{6,30},{7,31},{8,16},{9,... | collective-permute-start | bytes 196616 | tf_op jit(solution)/shard_map/ppermute | solution.py:233
  47.3 4.6 %collective-permute-start.12 = (bf16[8,32,128]{2,1,0:T(8,128)(2,1)S(1)}, bf16[8,32,128]{2,1,0:T(8,128)(2,1)S(1)}, u32[]{:S(2)}, u32[]{:S(2)}) collective-permute-start(bf16[8,32,128]{2,1,0:T(8,128)(2,1)S(1)} %shard_map.79), channel_id=1, source_target_pairs={{0,8},{1,9},{2,10},{3,11},{4,12},{5,13},{6,14},{7,15},{8,0},{9,1},... | collective-permute-start | bytes 196616 | tf_op jit(solution)/shard_map/ppermute | solution.py:233
  47.4 5.9 %collective-permute-start.15 = (bf16[8,32,128]{2,1,0:T(8,128)(2,1)S(1)}, bf16[8,32,128]{2,1,0:T(8,128)(2,1)S(1)}, u32[]{:S(2)}, u32[]{:S(2)}) collective-permute-start(bf16[8,32,128]{2,1,0:T(8,128)(2,1)S(1)} %shard_map.81), channel_id=1, source_target_pairs={{0,16},{1,17},{2,18},{3,19},{4,20},{5,21},{6,22},{7,23},{8,24},{9,... | collective-permute-start | bytes 196616 | tf_op jit(solution)/shard_map/ppermute | solution.py:233
  50.2 6.1 %collective-permute-start.18 = (bf16[8,32,128]{2,1,0:T(8,128)(2,1)S(1)}, bf16[8,32,128]{2,1,0:T(8,128)(2,1)S(1)}, u32[]{:S(2)}, u32[]{:S(2)}) collective-permute-start(bf16[8,32,128]{2,1,0:T(8,128)(2,1)S(1)} %shard_map.83), channel_id=1, source_target_pairs={{0,24},{1,25},{2,26},{3,27},{4,28},{5,29},{6,30},{7,31},{8,16},{9,... | collective-permute-start | bytes 196616 | tf_op jit(solution)/shard_map/ppermute | solution.py:233
where the time goes:
time: 57.4 us; the launch traced here: 57.2 us
  starting transfers between devices  30 us (52%)
  waiting for transfers between devices  19.6 us (34%)
  Pallas kernels  6.02 us (10%)
  local copies, waits for them, and re-layouts  0.79 us (1%)
  between operations  0.79 us (1%)
    ppermute x20, starting transfers between devices, send(): return lax.ppermute(value, AXES, pairs)  30 us
    ppermute x20, waiting for transfers between devices, send(): return lax.ppermute(value, AXES, pairs)  19.6 us
    pallas_call x18, Pallas kernels, kernel_call(): pl.pallas_call(body, out_shape=shapes, in_specs=[near] * len(args), out_s...  6.02 us
  transfers between devices with their start and end apart: 20, of which 8 were waited for; matrix products, arithmetic and copies ran while one was open for 0% of the time, Pallas kernels for 5%

commit v1 on v0

--- a/solution.py
+++ b/solution.py
@@ -37,16 +37,20 @@
     return pl.ds(pl.multiple_of(slot * n, n), n)
 
 
-def kernel_call(body, outs, scratch, flops, args):
+def kernel_call(body, outs, scratch, flops, args, place_out=pltpu.VMEM):
     shapes = [jax.ShapeDtypeStruct(*o) for o in outs]
     moved = sum(a.size * a.dtype.itemsize for a in (*args, *shapes))
-    held = sum(math.prod(m.shape) * jnp.dtype(m.dtype).itemsize for m in scratch)
+    held = sum(
+        math.prod(m.shape) * jnp.dtype(m.dtype).itemsize
+        for m in scratch
+        if m.memory_space == pltpu.VMEM
+    )
     near = pl.BlockSpec(memory_space=pltpu.VMEM)
     return pl.pallas_call(
         body,
         out_shape=shapes,
         in_specs=[near] * len(args),
-        out_specs=[near] * len(outs),
+        out_specs=[pl.BlockSpec(memory_space=place_out)] * len(outs),
         scratch_shapes=scratch,
         compiler_params=pltpu.CompilerParams(vmem_limit_bytes=moved + held + SPARE),
         cost_estimate=pl.CostEstimate(
@@ -201,19 +205,24 @@
 
 
 def finish_body(count, parts, *refs):
-    outs, wide = refs[-3:-1], refs[-1]
+    outs, (wide, staged, sems) = refs[-5:-3], refs[-3:]
     n, freqs, width = outs[0].shape
-    groups = [refs[:count]] + [refs[count + q : -3 : parts] for q in range(parts)]
-    for out, sets in ((outs[0], groups[:1]), (outs[1], groups[1:])):
+    copies = []
+    groups = [refs[:count]] + [refs[count + q : -5 : parts] for q in range(parts)]
+    for which, sets in enumerate((groups[:1], groups[1:])):
         f = 0
         for terms in sets:
             for i in range(terms[0].shape[0]):
                 total = 0.0
                 for term in terms:
                     total += term[i, :n].astype(F32)
-                wide[pl.ds(f, n, stride=freqs), :] = total
+                wide[which, pl.ds(f, n, stride=freqs), :] = total
                 f += 1
-        out[...] = wide[...].reshape(n, freqs, width).astype(BF16)
+        staged[which] = wide[which].reshape(n, freqs, width).astype(BF16)
+        copies.append(pltpu.make_async_copy(staged.at[which], outs[which], sems.at[which]))
+        copies[-1].start()
+    for copy in copies:
+        copy.wait()
 
 
 def per_device(row_count, cols, spectra, window_flags, pair_mask, misfit_weight, observed):
@@ -235,9 +244,7 @@
     def piece(size, count=1):
         return ((size, count * n, width), BF16)
 
-    (both,) = kernel_call(
-        bits_body, [((n, width), F32)], [], WAIT_FLOPS, (window_flags,)
-    )
+    (both,) = kernel_call(bits_body, [((n, width), F32)], [], WAIT_FLOPS, (window_flags,))
     (own,) = kernel_call(
         flag_body,
         [piece(freqs)],
@@ -253,15 +260,10 @@
         own.size,
         (own, mate),
     )
-    side = [chip] + [
-        send(chip, lambda z, t, c: (z, t, c ^ (2 * k))) for k in range(1, half)
-    ]
+    side = [chip] + [send(chip, lambda z, t, c: (z, t, c ^ (2 * k))) for k in range(1, half)]
     first_args, second_args = [], []
     for q, size in enumerate(sizes):
-        pieces = [
-            send(chips[q], lambda z, t, c: (spread(c, cols) ^ k, t, z))
-            for k in range(half)
-        ]
+        pieces = [send(chips[q], lambda z, t, c: (spread(c, cols) ^ k, t, z)) for k in range(half)]
         (stack,) = kernel_call(stack_body, [piece(size, cols)], [], own.size, pieces)
         for d in range(1, ratio):
             pieces.append(send(stack, lambda z, t, c: (z, t ^ d, c)))
@@ -327,9 +329,14 @@
     grad_first, grad_second = kernel_call(
         functools.partial(finish_body, len(first_terms), PARTS),
         [((n, freqs, width), BF16)] * 2,
-        [pltpu.VMEM((n * freqs, width), F32)],
+        [
+            pltpu.VMEM((2, n * freqs, width), F32),
+            pltpu.VMEM((2, n, freqs, width), BF16),
+            pltpu.SemaphoreType.DMA((2,)),
+        ],
         cols * spectra.size,
         first_terms + [term for terms in zip(*second_args) for term in terms],
+        pltpu.HBM,
     )
     return grad_first, grad_second[None]
 

time: 57.4 us -> 57.5 us (level)
  no operation moved by 1% of the time
where the time goes in v1:
time: 57.5 us; the launch traced here: 57.2 us
  starting transfers between devices  30 us (52%)
  waiting for transfers between devices  19.6 us (34%)
  Pallas kernels  6.03 us (10%)
  local copies, waits for them, and re-layouts  0.79 us (1%)
  between operations  0.79 us (1%)
    ppermute x20, starting transfers between devices, send(): return lax.ppermute(value, AXES, pairs)  30 us
    ppermute x20, waiting for transfers between devices, send(): return lax.ppermute(value, AXES, pairs)  19.6 us
    pallas_call x18, Pallas kernels, kernel_call(): pl.pallas_call(body, out_shape=shapes, in_specs=[near] * len(args), out_s...  6.03 us
  transfers between devices with their start and end apart: 20, of which 8 were waited for; matrix products, arithmetic and copies ran while one was open for 0% of the time, Pallas kernels for 5%

profile of v1, /device:TPU:0, one launch (start us, length us, event | category | flops | bytes accessed | tf_op | source)
XLA Modules:
  0.0 57.2 jit_solution(11633012760011459505)
XLA Ops:
  0.6 0.7 %copy-done.4 = s32[32,64]{1,0:T(8,128)S(1)} copy-done((s32[32,64]{1,0:T(8,128)S(1)}, s32[32,64]{1,0:T(8,128)}, u32[]{:S(2)}) %copy-start.4) | copy-done | bytes 8216
  1.7 0.6 collective-permute-start
  2.2 1.0 %collective-permute-done.mate = bf16[16,32,128]{2,1,0:T(8,128)(2,1)S(1)} collective-permute-done((bf16[16,32,128]{2,1,0:T(8,128)(2,1)S(1)}, bf16[16,32,128]{2,1,0:T(8,128)(2,1)S(1)}, u32[]{:S(2)}, u32[]{:S(2)}) %collective-permute-start) | collective-permute-done | bytes 131104 | tf_op jit(solution)/shard_map/ppermute | solution.py:242
  3.3 3.0 %collective-permute-start.6 = (bf16[8,64,128]{2,1,0:T(8,128)(2,1)S(1)}, bf16[8,64,128]{2,1,0:T(8,128)(2,1)S(1)}, u32[]{:S(2)}, u32[]{:S(2)}) collective-permute-start(bf16[8,64,128]{2,1,0:T(8,128)(2,1)S(1)} %get-tuple-element.33), channel_id=1, source_target_pairs={{0,8},{1,24},{2,0},{3,16},{4,12},{5,28},{6,4},{7,20},{8,9},{9,25},... | collective-permute-start | bytes 393224 | tf_op jit(solution)/shard_map/ppermute | solution.py:242
  6.3 0.7 %collective-permute-start.5 = (bf16[8,64,128]{2,1,0:T(8,128)(2,1)S(1)}, bf16[8,64,128]{2,1,0:T(8,128)(2,1)S(1)}, u32[]{:S(2)}, u32[]{:S(2)}) collective-permute-start(bf16[8,64,128]{2,1,0:T(8,128)(2,1)S(1)} %get-tuple-element.33), channel_id=1, source_target_pairs={{0,0},{1,16},{2,8},{3,24},{4,4},{5,20},{6,12},{7,28},{8,1},{9,17},... | collective-permute-start | bytes 393224 | tf_op jit(solution)/shard_map/ppermute | solution.py:242
  6.9 5.1 %collective-permute-start.2 = (bf16[8,64,128]{2,1,0:T(8,128)(2,1)S(1)}, bf16[8,64,128]{2,1,0:T(8,128)(2,1)S(1)}, u32[]{:S(2)}, u32[]{:S(2)}) collective-permute-start(bf16[8,64,128]{2,1,0:T(8,128)(2,1)S(1)} %get-tuple-element.28), channel_id=1, source_target_pairs={{0,8},{1,24},{2,0},{3,16},{4,12},{5,28},{6,4},{7,20},{8,9},{9,25},... | collective-permute-start | bytes 393224 | tf_op jit(solution)/shard_map/ppermute | solution.py:242
  12.0 0.7 %collective-permute-start.1 = (bf16[8,64,128]{2,1,0:T(8,128)(2,1)S(1)}, bf16[8,64,128]{2,1,0:T(8,128)(2,1)S(1)}, u32[]{:S(2)}, u32[]{:S(2)}) collective-permute-start(bf16[8,64,128]{2,1,0:T(8,128)(2,1)S(1)} %get-tuple-element.28), channel_id=1, source_target_pairs={{0,0},{1,16},{2,8},{3,24},{4,4},{5,20},{6,12},{7,28},{8,1},{9,17},... | collective-permute-start | bytes 393224 | tf_op jit(solution)/shard_map/ppermute | solution.py:242
  12.7 2.9 %collective-permute-start.4 = (bf16[16,64,128]{2,1,0:T(8,128)(2,1)S(1)}, bf16[16,64,128]{2,1,0:T(8,128)(2,1)S(1)}, u32[]{:S(2)}, u32[]{:S(2)}) collective-permute-start(bf16[16,64,128]{2,1,0:T(8,128)(2,1)S(1)} %get-tuple-element.29.refs_0_), channel_id=1, source_target_pairs={{0,2},{1,3},{2,0},{3,1},{4,6},{5,7},{6,4},{7,5},{8,10},{9,11},{10,... | collective-permute-start | bytes 786440 | tf_op jit(solution)/shard_map/ppermute | solution.py:242
  15.6 1.6 %collective-permute-start.7 = (bf16[8,128,128]{2,1,0:T(8,128)(2,1)S(1)}, bf16[8,128,128]{2,1,0:T(8,128)(2,1)S(1)}, u32[]{:S(2)}, u32[]{:S(2)}) collective-permute-start(bf16[8,128,128]{2,1,0:T(8,128)(2,1)S(1)} %shard_map.74), channel_id=1, source_target_pairs={{0,4},{1,5},{2,6},{3,7},{4,0},{5,1},{6,2},{7,3},{8,12},{9,13},{10,... | collective-permute-start | bytes 786440 | tf_op jit(solution)/shard_map/ppermute | solution.py:242
  17.2 0.6 collective-permute-start.3
  17.8 5.9 %collective-permute-done.4.refs_1_ = bf16[16,64,128]{2,1,0:T(8,128)(2,1)S(1)} collective-permute-done((bf16[16,64,128]{2,1,0:T(8,128)(2,1)S(1)}, bf16[16,64,128]{2,1,0:T(8,128)(2,1)S(1)}, u32[]{:S(2)}, u32[]{:S(2)}) %collective-permute-start.4) | collective-permute-done | bytes 262176 | tf_op jit(solution)/shard_map/ppermute | solution.py:242
  23.7 0.9 %shard_map.75 = (bf16[8,256,128]{2,1,0:T(8,128)(2,1)S(1)}, bf16[8,128,128]{2,1,0:T(8,128)(2,1)S(1)}) custom-call(bf16[16,64,128]{2,1,0:T(8,128)(2,1)S(1)} %get-tuple-element.29.refs_0_, bf16[16,64,128]{2,1,0:T(8,128)(2,1)S(1)} %collective-permute-done.4.refs_1_, bf16[8,64,128]{2,1,0:T(8,128)(2,1)S(1)} %collective-permute-done.5.refs_0_.refs_2_.refs_5_, ...), custom_call_target="tpu_custom_call" | custom-call | flops 134217728 | bytes 4849664 | tf_op jit(solution)/shard_map/pallas_call | solution.py:49
  24.6 0.9 %shard_map.72 = (bf16[8,256,128]{2,1,0:T(8,128)(2,1)S(1)}, bf16[8,128,128]{2,1,0:T(8,128)(2,1)S(1)}) custom-call(bf16[16,64,128]{2,1,0:T(8,128)(2,1)S(1)} %get-tuple-element.29.refs_0_, bf16[16,64,128]{2,1,0:T(8,128)(2,1)S(1)} %collective-permute-done.4.refs_1_, bf16[8,64,128]{2,1,0:T(8,128)(2,1)S(1)} %collective-permute-done.1.refs_0_.refs_2_, ...), custom_call_target="tpu_custom_call" | custom-call | flops 134217728 | bytes 4849664 | tf_op jit(solution)/shard_map/pallas_call | solution.py:49
  25.5 1.0 %shard_map.76 = (bf16[8,256,128]{2,1,0:T(8,128)(2,1)S(1)}, bf16[8,32,128]{2,1,0:T(8,128)(2,1)S(1)}, bf16[8,32,128]{2,1,0:T(8,128)(2,1)S(1)}, bf16[8,32,128]{2,1,...) custom-call(bf16[16,64,128]{2,1,0:T(8,128)(2,1)S(1)} %get-tuple-elem, ...), custom_call_target="tpu_custom_call" | custom-call | flops 134217728 | bytes 5373952 | tf_op jit(solution)/shard_map/pallas_call | solution.py:49
  26.5 2.5 %collective-permute-done.3.refs_2_ = bf16[8,128,128]{2,1,0:T(8,128)(2,1)S(1)} collective-permute-done((bf16[8,128,128]{2,1,0:T(8,128)(2,1)S(1)}, bf16[8,128,128]{2,1,0:T(8,128)(2,1)S(1)}, u32[]{:S(2)}, u32[]{:S(2)}) %collective-permute-start.3) | collective-permute-done | bytes 262176 | tf_op jit(solution)/shard_map/ppermute | solution.py:242
  29.0 1.0 %shard_map.73 = (bf16[8,256,128]{2,1,0:T(8,128)(2,1)S(1)}, bf16[8,32,128]{2,1,0:T(8,128)(2,1)S(1)}, bf16[8,32,128]{2,1,0:T(8,128)(2,1)S(1)}, bf16[8,32,128]{2,1,...) custom-call(bf16[16,64,128]{2,1,0:T(8,128)(2,1)S(1)} %get-tuple-elem, ...), custom_call_target="tpu_custom_call" | custom-call | flops 134217728 | bytes 5373952 | tf_op jit(solution)/shard_map/pallas_call | solution.py:49
  30.0 0.9 %shard_map.77 = (bf16[16,64,128]{2,1,0:T(8,128)(2,1)S(1)}, bf16[16,32,128]{2,1,0:T(8,128)(2,1)S(1)}, bf16[16,32,128]{2,1,0:T(8,128)(2,1)S(1)}) custom-call(bf16[8,64,128]{2,1,0:T(8,128)(2,1)S(1)} %collective-permute-done.1.refs_0_.refs_2_, bf16[8,64,128]{2,1,0:T(8,128)(2,1)S(1)} %collective-permute-done.2.refs_1_.refs_3_, ...), custom_call_target="tpu_custom_call" | custom-call | flops 268435456 | bytes 3670016 | tf_op jit(solution)/shard_map/pallas_call | solution.py:49
  30.9 1.4 %collective-permute-start.8 = (bf16[16,64,128]{2,1,0:T(8,128)(2,1)S(1)}, bf16[16,64,128]{2,1,0:T(8,128)(2,1)S(1)}, u32[]{:S(2)}, u32[]{:S(2)}) collective-permute-start(bf16[16,64,128]{2,1,0:T(8,128)(2,1)S(1)} %get-tuple-element.38), channel_id=1, source_target_pairs={{0,1},{1,0},{2,3},{3,2},{4,5},{5,4},{6,7},{7,6},{8,9},{9,8},{10,11... | collective-permute-start | bytes 786440 | tf_op jit(solution)/shard_map/ppermute | solution.py:242
  32.2 1.5 %collective-permute-start.11 = (bf16[8,64,128]{2,1,0:T(8,128)(2,1)S(1)}, bf16[8,64,128]{2,1,0:T(8,128)(2,1)S(1)}, u32[]{:S(2)}, u32[]{:S(2)}) collective-permute-start(bf16[8,64,128]{2,1,0:T(8,128)(2,1)S(1)} %get-tuple-element.43), channel_id=1, source_target_pairs={{0,4},{1,5},{2,6},{3,7},{4,0},{5,1},{6,2},{7,3},{8,12},{9,13},{10,... | collective-permute-start | bytes 393224 | tf_op jit(solution)/shard_map/ppermute | solution.py:242
  33.8 0.5 collective-permute-start.16
  34.3 1.5 %collective-permute-start.10 = (bf16[8,64,128]{2,1,0:T(8,128)(2,1)S(1)}, bf16[8,64,128]{2,1,0:T(8,128)(2,1)S(1)}, u32[]{:S(2)}, u32[]{:S(2)}) collective-permute-start(bf16[8,64,128]{2,1,0:T(8,128)(2,1)S(1)} %get-tuple-element.42), channel_id=1, source_target_pairs={{0,4},{1,5},{2,6},{3,7},{4,0},{5,1},{6,2},{7,3},{8,12},{9,13},{10,... | collective-permute-start | bytes 393224 | tf_op jit(solution)/shard_map/ppermute | solution.py:242
  35.8 0.5 collective-permute-start.14
  36.3 2.3 %collective-permute-done.11.refs_1_.refs_6_ = bf16[8,64,128]{2,1,0:T(8,128)(2,1)S(1)} collective-permute-done((bf16[8,64,128]{2,1,0:T(8,128)(2,1)S(1)}, bf16[8,64,128]{2,1,0:T(8,128)(2,1)S(1)}, u32[]{:S(2)}, u32[]{:S(2)}) %collective-permute-start.11) | collective-permute-done | bytes 131104 | tf_op jit(solution)/shard_map/ppermute | solution.py:242
  38.7 2.7 %collective-permute-done.16.refs_1_ = bf16[8,64,128]{2,1,0:T(8,128)(2,1)S(1)} collective-permute-done((bf16[8,64,128]{2,1,0:T(8,128)(2,1)S(1)}, bf16[8,64,128]{2,1,0:T(8,128)(2,1)S(1)}, u32[]{:S(2)}, u32[]{:S(2)}) %collective-permute-start.16) | collective-permute-done | bytes 131104 | tf_op jit(solution)/shard_map/ppermute | solution.py:242
  41.4 1.7 %collective-permute-start.17 = (bf16[8,32,128]{2,1,0:T(8,128)(2,1)S(1)}, bf16[8,32,128]{2,1,0:T(8,128)(2,1)S(1)}, u32[]{:S(2)}, u32[]{:S(2)}) collective-permute-start(bf16[8,32,128]{2,1,0:T(8,128)(2,1)S(1)} %shard_map.82), channel_id=1, source_target_pairs={{0,16},{1,17},{2,18},{3,19},{4,20},{5,21},{6,22},{7,23},{8,24},{9,... | collective-permute-start | bytes 196616 | tf_op jit(solution)/shard_map/ppermute | solution.py:242
  43.5 0.7 %collective-permute-done.10.refs_1_.refs_5_ = bf16[8,64,128]{2,1,0:T(8,128)(2,1)S(1)} collective-permute-done((bf16[8,64,128]{2,1,0:T(8,128)(2,1)S(1)}, bf16[8,64,128]{2,1,0:T(8,128)(2,1)S(1)}, u32[]{:S(2)}, u32[]{:S(2)}) %collective-permute-start.10) | collective-permute-done | bytes 131104 | tf_op jit(solution)/shard_map/ppermute | solution.py:242
  44.2 3.0 %collective-permute-start.19 = (bf16[8,32,128]{2,1,0:T(8,128)(2,1)S(1)}, bf16[8,32,128]{2,1,0:T(8,128)(2,1)S(1)}, u32[]{:S(2)}, u32[]{:S(2)}) collective-permute-start(bf16[8,32,128]{2,1,0:T(8,128)(2,1)S(1)} %shard_map.84), channel_id=1, source_target_pairs={{0,24},{1,25},{2,26},{3,27},{4,28},{5,29},{6,30},{7,31},{8,16},{9,... | collective-permute-start | bytes 196616 | tf_op jit(solution)/shard_map/ppermute | solution.py:242
  47.4 2.8 %collective-permute-start.15 = (bf16[8,32,128]{2,1,0:T(8,128)(2,1)S(1)}, bf16[8,32,128]{2,1,0:T(8,128)(2,1)S(1)}, u32[]{:S(2)}, u32[]{:S(2)}) collective-permute-start(bf16[8,32,128]{2,1,0:T(8,128)(2,1)S(1)} %shard_map.81), channel_id=1, source_target_pairs={{0,16},{1,17},{2,18},{3,19},{4,20},{5,21},{6,22},{7,23},{8,24},{9,... | collective-permute-start | bytes 196616 | tf_op jit(solution)/shard_map/ppermute | solution.py:242
  50.2 1.7 %collective-permute-start.18 = (bf16[8,32,128]{2,1,0:T(8,128)(2,1)S(1)}, bf16[8,32,128]{2,1,0:T(8,128)(2,1)S(1)}, u32[]{:S(2)}, u32[]{:S(2)}) collective-permute-start(bf16[8,32,128]{2,1,0:T(8,128)(2,1)S(1)} %shard_map.83), channel_id=1, source_target_pairs={{0,24},{1,25},{2,26},{3,27},{4,28},{5,29},{6,30},{7,31},{8,16},{9,... | collective-permute-start | bytes 196616 | tf_op jit(solution)/shard_map/ppermute | solution.py:242
  51.9 1.4 %collective-permute-done.15.refs_9_ = bf16[8,32,128]{2,1,0:T(8,128)(2,1)S(1)} collective-permute-done((bf16[8,32,128]{2,1,0:T(8,128)(2,1)S(1)}, bf16[8,32,128]{2,1,0:T(8,128)(2,1)S(1)}, u32[]{:S(2)}, u32[]{:S(2)}) %collective-permute-start.15) | collective-permute-done | bytes 65568 | tf_op jit(solution)/shard_map/ppermute | solution.py:242
  53.3 2.9 %collective-permute-done.18.refs_11_ = bf16[8,32,128]{2,1,0:T(8,128)(2,1)S(1)} collective-permute-done((bf16[8,32,128]{2,1,0:T(8,128)(2,1)S(1)}, bf16[8,32,128]{2,1,0:T(8,128)(2,1)S(1)}, u32[]{:S(2)}, u32[]{:S(2)}) %collective-permute-start.18) | collective-permute-done | bytes 65568 | tf_op jit(solution)/shard_map/ppermute | solution.py:242
  56.2 0.9 %shard_map.85 = (bf16[32,16,128]{2,1,0:T(8,128)(2,1)}, bf16[32,16,128]{2,1,0:T(8,128)(2,1)}) custom-call(bf16[16,32,128]{2,1,0:T(8,128)(2,1)S(1)} %get-tuple-element.37.refs_0_, bf16[16,64,128]{2,1,0:T(8,128)(2,1)S(1)} %collective-permute-done.8.refs_1_, bf16[16,32,128]{2,1,0:T(8,128)(2,1)S(1)} %collective-permute-done.9.refs_2_, ...), custom_call_target="tpu_custom_call" | custom-call | flops 262144 | bytes 1572864 | tf_op jit(solution)/shard_map/pallas_call | solution.py:49
  (36 shorter events, 1.0 us)
Async XLA Ops:
  0.6 0.9 %copy-start.3 = (bf16[32,16,128]{2,1,0:T(8,128)(2,1)S(1)}, bf16[32,16,128]{2,1,0:T(8,128)(2,1)}, u32[]{:S(2)}) copy-start(bf16[32,16,128]{2,1,0:T(8,128)(2,1)} %spectra.1) | copy-start | bytes 393220
  0.6 0.8 %copy-start.4 = (s32[32,64]{1,0:T(8,128)S(1)}, s32[32,64]{1,0:T(8,128)}, u32[]{:S(2)}) copy-start(s32[32,64]{1,0:T(8,128)} %flags.1) | copy-start | bytes 24580
  1.6 22.2 %copy-start = (bf16[2,16,128,256]{3,2,1,0:T(8,128)(2,1)S(1)}, bf16[2,16,128,256]{3,2,1,0:T(8,128)(2,1)}, u32[]{:S(2)}) copy-start(bf16[2,16,128,256]{3,2,1,0:T(8,128)(2,1)} %refs_5_.7) | copy-start | bytes 6291460
  1.6 22.2 %copy-start.1 = (bf16[16,128,256]{2,1,0:T(8,128)(2,1)S(1)}, bf16[16,128,256]{2,1,0:T(8,128)(2,1)}, u32[]{:S(2)}) copy-start(bf16[16,128,256]{2,1,0:T(8,128)(2,1)} %refs_4_.7) | copy-start | bytes 3145732
  1.6 22.2 %copy-start.2 = (s32[128,256]{1,0:T(8,128)S(1)}, s32[128,256]{1,0:T(8,128)}, u32[]{:S(2)}) copy-start(s32[128,256]{1,0:T(8,128)} %refs_3_.3) | copy-start | bytes 393220
  1.7 1.5 %collective-permute-start = (bf16[16,32,128]{2,1,0:T(8,128)(2,1)S(1)}, bf16[16,32,128]{2,1,0:T(8,128)(2,1)S(1)}, u32[]{:S(2)}, u32[]{:S(2)}) collective-permute-start(bf16[16,32,128]{2,1,0:T(8,128)(2,1)S(1)} %shard_map.69.own), channel_id=1, source_target_pairs={{0,1},{1,0},{2,3},{3,2},{4,5},{5,4},{6,7},{7,6},{8,9},{9,8},{10,11... | collective-permute-start | bytes 393224 | tf_op jit(solution)/shard_map/ppermute | solution.py:242
  3.3 12.3 %collective-permute-start.6 = (bf16[8,64,128]{2,1,0:T(8,128)(2,1)S(1)}, bf16[8,64,128]{2,1,0:T(8,128)(2,1)S(1)}, u32[]{:S(2)}, u32[]{:S(2)}) collective-permute-start(bf16[8,64,128]{2,1,0:T(8,128)(2,1)S(1)} %get-tuple-element.33), channel_id=1, source_target_pairs={{0,8},{1,24},{2,0},{3,16},{4,12},{5,28},{6,4},{7,20},{8,9},{9,25},... | collective-permute-start | bytes 393224 | tf_op jit(solution)/shard_map/ppermute | solution.py:242
  6.3 9.3 %collective-permute-start.5 = (bf16[8,64,128]{2,1,0:T(8,128)(2,1)S(1)}, bf16[8,64,128]{2,1,0:T(8,128)(2,1)S(1)}, u32[]{:S(2)}, u32[]{:S(2)}) collective-permute-start(bf16[8,64,128]{2,1,0:T(8,128)(2,1)S(1)} %get-tuple-element.33), channel_id=1, source_target_pairs={{0,0},{1,16},{2,8},{3,24},{4,4},{5,20},{6,12},{7,28},{8,1},{9,17},... | collective-permute-start | bytes 393224 | tf_op jit(solution)/shard_map/ppermute | solution.py:242
  6.9 10.3 %collective-permute-start.2 = (bf16[8,64,128]{2,1,0:T(8,128)(2,1)S(1)}, bf16[8,64,128]{2,1,0:T(8,128)(2,1)S(1)}, u32[]{:S(2)}, u32[]{:S(2)}) collective-permute-start(bf16[8,64,128]{2,1,0:T(8,128)(2,1)S(1)} %get-tuple-element.28), channel_id=1, source_target_pairs={{0,8},{1,24},{2,0},{3,16},{4,12},{5,28},{6,4},{7,20},{8,9},{9,25},... | collective-permute-start | bytes 393224 | tf_op jit(solution)/shard_map/ppermute | solution.py:242
  12.0 5.2 %collective-permute-start.1 = (bf16[8,64,128]{2,1,0:T(8,128)(2,1)S(1)}, bf16[8,64,128]{2,1,0:T(8,128)(2,1)S(1)}, u32[]{:S(2)}, u32[]{:S(2)}) collective-permute-start(bf16[8,64,128]{2,1,0:T(8,128)(2,1)S(1)} %get-tuple-element.28), channel_id=1, source_target_pairs={{0,0},{1,16},{2,8},{3,24},{4,4},{5,20},{6,12},{7,28},{8,1},{9,17},... | collective-permute-start | bytes 393224 | tf_op jit(solution)/shard_map/ppermute | solution.py:242
  12.7 11.1 %collective-permute-start.4 = (bf16[16,64,128]{2,1,0:T(8,128)(2,1)S(1)}, bf16[16,64,128]{2,1,0:T(8,128)(2,1)S(1)}, u32[]{:S(2)}, u32[]{:S(2)}) collective-permute-start(bf16[16,64,128]{2,1,0:T(8,128)(2,1)S(1)} %get-tuple-element.29.refs_0_), channel_id=1, source_target_pairs={{0,2},{1,3},{2,0},{3,1},{4,6},{5,7},{6,4},{7,5},{8,10},{9,11},{10,... | collective-permute-start | bytes 786440 | tf_op jit(solution)/shard_map/ppermute | solution.py:242
  15.6 9.9 %collective-permute-start.7 = (bf16[8,128,128]{2,1,0:T(8,128)(2,1)S(1)}, bf16[8,128,128]{2,1,0:T(8,128)(2,1)S(1)}, u32[]{:S(2)}, u32[]{:S(2)}) collective-permute-start(bf16[8,128,128]{2,1,0:T(8,128)(2,1)S(1)} %shard_map.74), channel_id=1, source_target_pairs={{0,4},{1,5},{2,6},{3,7},{4,0},{5,1},{6,2},{7,3},{8,12},{9,13},{10,... | collective-permute-start | bytes 786440 | tf_op jit(solution)/shard_map/ppermute | solution.py:242
  17.2 11.8 %collective-permute-start.3 = (bf16[8,128,128]{2,1,0:T(8,128)(2,1)S(1)}, bf16[8,128,128]{2,1,0:T(8,128)(2,1)S(1)}, u32[]{:S(2)}, u32[]{:S(2)}) collective-permute-start(bf16[8,128,128]{2,1,0:T(8,128)(2,1)S(1)} %shard_map.71), channel_id=1, source_target_pairs={{0,4},{1,5},{2,6},{3,7},{4,0},{5,1},{6,2},{7,3},{8,12},{9,13},{10,... | collective-permute-start | bytes 786440 | tf_op jit(solution)/shard_map/ppermute | solution.py:242
  30.9 12.3 %collective-permute-start.8 = (bf16[16,64,128]{2,1,0:T(8,128)(2,1)S(1)}, bf16[16,64,128]{2,1,0:T(8,128)(2,1)S(1)}, u32[]{:S(2)}, u32[]{:S(2)}) collective-permute-start(bf16[16,64,128]{2,1,0:T(8,128)(2,1)S(1)} %get-tuple-element.38), channel_id=1, source_target_pairs={{0,1},{1,0},{2,3},{3,2},{4,5},{5,4},{6,7},{7,6},{8,9},{9,8},{10,11... | collective-permute-start | bytes 786440 | tf_op jit(solution)/shard_map/ppermute | solution.py:242
  32.2 6.4 %collective-permute-start.11 = (bf16[8,64,128]{2,1,0:T(8,128)(2,1)S(1)}, bf16[8,64,128]{2,1,0:T(8,128)(2,1)S(1)}, u32[]{:S(2)}, u32[]{:S(2)}) collective-permute-start(bf16[8,64,128]{2,1,0:T(8,128)(2,1)S(1)} %get-tuple-element.43), channel_id=1, source_target_pairs={{0,4},{1,5},{2,6},{3,7},{4,0},{5,1},{6,2},{7,3},{8,12},{9,13},{10,... | collective-permute-start | bytes 393224 | tf_op jit(solution)/shard_map/ppermute | solution.py:242
  33.8 7.7 %collective-permute-start.16 = (bf16[8,64,128]{2,1,0:T(8,128)(2,1)S(1)}, bf16[8,64,128]{2,1,0:T(8,128)(2,1)S(1)}, u32[]{:S(2)}, u32[]{:S(2)}) collective-permute-start(bf16[8,64,128]{2,1,0:T(8,128)(2,1)S(1)} %get-tuple-element.49), channel_id=1, source_target_pairs={{0,4},{1,5},{2,6},{3,7},{4,0},{5,1},{6,2},{7,3},{8,12},{9,13},{10,... | collective-permute-start | bytes 393224 | tf_op jit(solution)/shard_map/ppermute | solution.py:242
  34.3 10.0 %collective-permute-start.10 = (bf16[8,64,128]{2,1,0:T(8,128)(2,1)S(1)}, bf16[8,64,128]{2,1,0:T(8,128)(2,1)S(1)}, u32[]{:S(2)}, u32[]{:S(2)}) collective-permute-start(bf16[8,64,128]{2,1,0:T(8,128)(2,1)S(1)} %get-tuple-element.42), channel_id=1, source_target_pairs={{0,4},{1,5},{2,6},{3,7},{4,0},{5,1},{6,2},{7,3},{8,12},{9,13},{10,... | collective-permute-start | bytes 393224 | tf_op jit(solution)/shard_map/ppermute | solution.py:242
  35.8 11.5 %collective-permute-start.14 = (bf16[8,64,128]{2,1,0:T(8,128)(2,1)S(1)}, bf16[8,64,128]{2,1,0:T(8,128)(2,1)S(1)}, u32[]{:S(2)}, u32[]{:S(2)}) collective-permute-start(bf16[8,64,128]{2,1,0:T(8,128)(2,1)S(1)} %get-tuple-element.47), channel_id=1, source_target_pairs={{0,4},{1,5},{2,6},{3,7},{4,0},{5,1},{6,2},{7,3},{8,12},{9,13},{10,... | collective-permute-start | bytes 393224 | tf_op jit(solution)/shard_map/ppermute | solution.py:242
  38.6 8.8 %collective-permute-start.13 = (bf16[8,32,128]{2,1,0:T(8,128)(2,1)S(1)}, bf16[8,32,128]{2,1,0:T(8,128)(2,1)S(1)}, u32[]{:S(2)}, u32[]{:S(2)}) collective-permute-start(bf16[8,32,128]{2,1,0:T(8,128)(2,1)S(1)} %shard_map.80), channel_id=1, source_target_pairs={{0,8},{1,9},{2,10},{3,11},{4,12},{5,13},{6,14},{7,15},{8,0},{9,1},... | collective-permute-start | bytes 196616 | tf_op jit(solution)/shard_map/ppermute | solution.py:242
  41.4 8.7 %collective-permute-start.17 = (bf16[8,32,128]{2,1,0:T(8,128)(2,1)S(1)}, bf16[8,32,128]{2,1,0:T(8,128)(2,1)S(1)}, u32[]{:S(2)}, u32[]{:S(2)}) collective-permute-start(bf16[8,32,128]{2,1,0:T(8,128)(2,1)S(1)} %shard_map.82), channel_id=1, source_target_pairs={{0,16},{1,17},{2,18},{3,19},{4,20},{5,21},{6,22},{7,23},{8,24},{9,... | collective-permute-start | bytes 196616 | tf_op jit(solution)/shard_map/ppermute | solution.py:242
  43.2 13.0 %collective-permute-start.9 = (bf16[16,32,128]{2,1,0:T(8,128)(2,1)S(1)}, bf16[16,32,128]{2,1,0:T(8,128)(2,1)S(1)}, u32[]{:S(2)}, u32[]{:S(2)}) collective-permute-start(bf16[16,32,128]{2,1,0:T(8,128)(2,1)S(1)} %shard_map.78), channel_id=1, source_target_pairs={{0,2},{1,3},{2,0},{3,1},{4,6},{5,7},{6,4},{7,5},{8,10},{9,11},{10,... | collective-permute-start | bytes 393224 | tf_op jit(solution)/shard_map/ppermute | solution.py:242
  44.2 7.6 %collective-permute-start.19 = (bf16[8,32,128]{2,1,0:T(8,128)(2,1)S(1)}, bf16[8,32,128]{2,1,0:T(8,128)(2,1)S(1)}, u32[]{:S(2)}, u32[]{:S(2)}) collective-permute-start(bf16[8,32,128]{2,1,0:T(8,128)(2,1)S(1)} %shard_map.84), channel_id=1, source_target_pairs={{0,24},{1,25},{2,26},{3,27},{4,28},{5,29},{6,30},{7,31},{8,16},{9,... | collective-permute-start | bytes 196616 | tf_op jit(solution)/shard_map/ppermute | solution.py:242
  47.3 4.6 %collective-permute-start.12 = (bf16[8,32,128]{2,1,0:T(8,128)(2,1)S(1)}, bf16[8,32,128]{2,1,0:T(8,128)(2,1)S(1)}, u32[]{:S(2)}, u32[]{:S(2)}) collective-permute-start(bf16[8,32,128]{2,1,0:T(8,128)(2,1)S(1)} %shard_map.79), channel_id=1, source_target_pairs={{0,8},{1,9},{2,10},{3,11},{4,12},{5,13},{6,14},{7,15},{8,0},{9,1},... | collective-permute-start | bytes 196616 | tf_op jit(solution)/shard_map/ppermute | solution.py:242
  47.4 5.9 %collective-permute-start.15 = (bf16[8,32,128]{2,1,0:T(8,128)(2,1)S(1)}, bf16[8,32,128]{2,1,0:T(8,128)(2,1)S(1)}, u32[]{:S(2)}, u32[]{:S(2)}) collective-permute-start(bf16[8,32,128]{2,1,0:T(8,128)(2,1)S(1)} %shard_map.81), channel_id=1, source_target_pairs={{0,16},{1,17},{2,18},{3,19},{4,20},{5,21},{6,22},{7,23},{8,24},{9,... | collective-permute-start | bytes 196616 | tf_op jit(solution)/shard_map/ppermute | solution.py:242
  50.2 6.1 %collective-permute-start.18 = (bf16[8,32,128]{2,1,0:T(8,128)(2,1)S(1)}, bf16[8,32,128]{2,1,0:T(8,128)(2,1)S(1)}, u32[]{:S(2)}, u32[]{:S(2)}) collective-permute-start(bf16[8,32,128]{2,1,0:T(8,128)(2,1)S(1)} %shard_map.83), channel_id=1, source_target_pairs={{0,24},{1,25},{2,26},{3,27},{4,28},{5,29},{6,30},{7,31},{8,16},{9,... | collective-permute-start | bytes 196616 | tf_op jit(solution)/shard_map/ppermute | solution.py:242
